TPU v7x, 32 devices: a whole 2x2x4 slice. The times are simulated.
32 devices in a mesh: mp: 8 (over z, y), rows: 4 (over x, core).
Axes of the slice: x: 2, y: 2, z: 4, core: 2. Of those that a mesh axis runs over, the one named last changes fastest.
Arguments:
- inputs: float32 [1024, 16384], P('rows', 'mp'), may hold values from -6 to 6
- weight: float32 [512, 16384], P('mp'), may hold values from -1.5 to 1.5, as said below
Outputs:
- row_scale: float32 [1024], P('rows')
- product: float32 [512, 1024], P('mp', 'rows')
- normalized: float32 [512, 1024], P('mp')
Inputs may be any that keep to these rules, and one draw needn't show every extreme that they name: A weight matrix whose rows carry different scales.
All inputs are finite; a program needn't handle non-finite values. Where the computation divides by a largest or mean magnitude, that divisor is 1e-20 or more.
Results may differ from a plain program's by a relative error of at most 0.0003.
Values may be sent and summed in bfloat16 or wider, within the bound.
No kernel may reach another device: no remote copies, remote signals or barrier semaphores. Data moves between devices by JAX's collectives and lax.ppermute only.
A program may use at most 64 MiB of HBM per device.

v0:
```python
import jax
import jax.numpy as jnp
from jax import lax
from jax.sharding import PartitionSpec as P

epsilon = 1e-06


def split_two(values):
    scaled = values * 128.0
    first = jnp.floor(scaled)
    second = jnp.floor((scaled - first) * 256.0)
    return (first.astype(jnp.bfloat16), second.astype(jnp.bfloat16))


def matmul(w_side, x_side):
    return lax.dot_general(
        w_side, x_side, (((1,), (1,)), ((), ())), preferred_element_type=jnp.float32
    )


def pair_sums(x_parts, w_parts):
    level_zero = matmul(w_parts[0], x_parts[0])
    level_one = matmul(w_parts[0], x_parts[1]) + matmul(w_parts[1], x_parts[0])
    return (level_zero, level_one)


def combine_levels(levels):
    return levels[0] + levels[1] / 256.0


def per_device(inputs, weight):
    col_scale = jnp.max(jnp.abs(weight), axis=1) + epsilon
    w_parts = split_two(weight / col_scale[:, None])
    row_scale = lax.pmax(jnp.max(jnp.abs(inputs), axis=1), "mp") + epsilon
    x_parts = split_two(inputs / row_scale[:, None])
    stacked = jnp.stack(w_parts, axis=0)
    moved = lax.all_to_all(stacked, "mp", split_axis=2, concat_axis=1, tiled=True)
    partial_term = combine_levels(pair_sums(x_parts, (moved[0], moved[1])))
    combined = lax.psum_scatter(partial_term, "mp", scatter_dimension=0, tiled=True)
    product = combined * col_scale[:, None] * row_scale[None, :] / 16384.0
    squares = lax.psum(jnp.sum(product * product, axis=0), "mp")
    mean_square = squares / (weight.shape[0] * lax.axis_size("mp"))
    normalized = product * lax.rsqrt(mean_square + epsilon)[None, :]
    gathered_rows = lax.all_gather(normalized, "rows", axis=1, tiled=True)
    return (row_scale, product, gathered_rows)


def solution(mesh):
    return jax.shard_map(
        per_device,
        mesh=mesh,
        in_specs=(P("rows", "mp"), P("mp", None)),
        out_specs=(P("rows"), P("mp", "rows"), P("mp", None)),
        check_vma=False,
    )
```

profile of v0, /device:TPU:0, one launch (start us, length us, event | category | flops | bytes accessed | tf_op | source)
XLA Modules:
  0.0 281.4 jit_solution(13112939245431465066)
XLA Ops:
  7.2 0.0 copy-start
  7.2 2.6 abs_reduce_fusion
  9.8 0.8 copy-done
  10.6 1.1 fusion.7
  11.7 2.3 pad_maximum_fusion
  14.0 17.8 %copy.12 = bf16[2,64,16384]{1,0,2:T(2,128)(2,1)} copy(bf16[2,64,16384]{2,1,0:T(8,128)(2,1)} %pad_maximum_fusion) | data formatting | bytes 8388608 | tf_op jit(solution)/shard_map/stack | solution.py:37
  31.8 10.5 %reshape.16 = bf16[8,2,131072]{2,1,0:T(2,128)(2,1)} reshape(bf16[16384,2,64]{2,1,0:T(2,128)(2,1)} %bitcast.13) | data formatting | bytes 8388608
  42.3 0.0 copy-start.1
  42.3 7.4 %all-to-all-start = ((bf16[8,2,131072]{2,1,0:T(2,128)(2,1)}), bf16[8,2,131072]{2,1,0:T(2,128)(2,1)}, u32[]{:S(2)}, u32[]{:S(2)}) async-start(bf16[8,2,131072]{2,1,0:T(2,128)(2,1)} %reshape.16), calls=%async_computation | async-start | bytes 8388608 | tf_op jit(solution)/shard_map/all_to_all | solution.py:38
  49.7 0.0 reduce-scatter.2.cloned.1.call-start
  49.8 0.0 copy-done.1
  49.8 0.2 abs_reduce_fusion.1
  50.0 85.0 %pmax.7 = f32[256]{0:T(256)S(1)} all-reduce(f32[256]{0:T(256)S(1)} %abs_reduce_fusion.1), channel_id=1, replica_groups=mesh['mp'=8,'rows'=4] {'mp'}, use_global_device_ids=true, to_apply=%region_1.0 | all-reduce | flops 256 | bytes 2048 | tf_op jit(solution)/shard_map/pmax | solution.py:35
  135.0 0.0 copy-start.2
  135.0 8.1 %all-to-all-done = bf16[8,2,131072]{2,1,0:T(2,128)(2,1)} async-done(((bf16[8,2,131072]{2,1,0:T(2,128)(2,1)}), bf16[8,2,131072]{2,1,0:T(2,128)(2,1)}, u32[]{:S(2)}, u32[]{:S(2)}) %all-to-all-start) | async-done | bytes 4194336 | tf_op jit(solution)/shard_map/all_to_all | solution.py:38
  143.1 10.3 %reshape.17 = bf16[16384,2,64]{2,1,0:T(2,128)(2,1)} reshape(bf16[8,2,131072]{2,1,0:T(2,128)(2,1)} %all-to-all-done) | data formatting | bytes 8388608
  153.4 13.6 %copy.16 = bf16[2,64,8,2048]{3,2,1,0:T(8,128)(2,1)} copy(bf16[2,64,8,2048]{1,0,3,2:T(2,128)(2,1)} %bitcast.14) | data formatting | bytes 8388608 | tf_op jit(solution)/shard_map/all_to_all | solution.py:38
  167.0 2.7 fusion.16
  169.7 1.2 copy.14
  170.9 1.2 copy.15
  172.1 1.0 fusion.9
  173.1 0.9 fusion.8
  174.0 1.7 convolution_add_fusion.1
  175.6 0.0 reduce-scatter.2.cloned.1.call-update
  175.6 70.5 %reduce-scatter.2.cloned.1.call-done = f32[64,256]{1,0:T(8,128)} async-done(((f32[512,256]{1,0:T(8,128)}), f32[64,256]{1,0:T(8,128)}) %reduce-scatter.2.cloned.1.call-update) | async-done | bytes 65552 | tf_op jit(solution)/shard_map/reduce_scatter | solution.py:40
  246.1 1.6 multiply_reduce_fusion
  247.7 19.4 %psum.7 = f32[256]{0:T(256)S(1)} all-reduce(f32[256]{0:T(256)S(1)} %get-tuple-element.3), channel_id=1, replica_groups=mesh['mp'=8,'rows'=4] {'mp'}, use_global_device_ids=true, to_apply=%region_5.0 | all-reduce | flops 256 | bytes 2048 | tf_op jit(solution)/shard_map/psum | solution.py:42
  267.1 0.0 copy-done.2
  267.1 0.9 fusion.12
  268.0 5.8 %all_gather.3 = f32[64,1024]{1,0:T(8,128)S(1)} all-gather(f32[64,256]{1,0:T(8,128)S(1)} %fusion.12), channel_id=1, replica_groups=mesh['mp'=8,'rows'=4] {'rows'}, dimensions={1}, use_global_device_ids=true | all-gather | bytes 327680 | tf_op jit(solution)/shard_map/all_gather | solution.py:45
  273.8 0.7 copy.18
  (3 shorter events, 0.0 us)
Async XLA Ops:
  7.2 3.5 %copy-start = (f32[64,16384]{1,0:T(8,128)S(1)}, f32[64,16384]{1,0:T(8,128)}, u32[]{:S(2)}) copy-start(f32[64,16384]{1,0:T(8,128)} %param.3) | copy-start | bytes 12582916
  42.3 7.5 %copy-start.1 = (f32[256,2048]{1,0:T(8,128)S(1)}, f32[256,2048]{1,0:T(8,128)}, u32[]{:S(2)}) copy-start(f32[256,2048]{1,0:T(8,128)} %param.2) | copy-start | bytes 6291460
  42.3 100.8 %all-to-all-start = ((bf16[8,2,131072]{2,1,0:T(2,128)(2,1)}), bf16[8,2,131072]{2,1,0:T(2,128)(2,1)}, u32[]{:S(2)}, u32[]{:S(2)}) async-start(bf16[8,2,131072]{2,1,0:T(2,128)(2,1)} %reshape.16), calls=%async_computation | async-start | bytes 8388608 | tf_op jit(solution)/shard_map/all_to_all | solution.py:38
  49.7 196.4 %reduce-scatter.2.cloned.1.call-start = ((), (), s32[]{:S(2)}) async-start(), calls=%async_computation.2 | async-start | bytes 589824 | tf_op jit(solution)/shard_map/reduce_scatter | solution.py:40
  135.0 132.1 %copy-start.2 = (f32[256]{0:T(256)}, f32[256]{0:T(256)S(1)}, u32[]{:S(2)}) copy-start(f32[256]{0:T(256)S(1)} %broadcast_add_fusion) | copy-start | bytes 3076
Sparse Core Ops, SparseCore 0:
  175.8 70.3 reduce-scatter.1
where the time goes:
time: 283 us; the launch traced here: 281 us
  blocking collectives  110 us (39%)
  waiting for transfers between devices  78.6 us (28%)
  local copies, waits for them, and re-layouts  58.7 us (21%)
  between operations  14.1 us (5%)
  other arithmetic  8.76 us (3%)
  starting transfers between devices  7.48 us (3%)
  matrix products  3.54 us (1%)
    pmax x1, blocking collectives, per_device(): row_scale = lax.pmax(jnp.max(jnp.abs(inputs), axis=1), 'mp') + epsilon  85 us
    reduce_scatter x1, waiting for transfers between devices, per_device(): lax.psum_scatter(partial_term, 'mp', scatter_dimension=0, tiled=True)  70.5 us
    unnamed x9, local copies, waits for them, and re-layouts  22.3 us
    psum x1, blocking collectives, per_device(): squares = lax.psum(jnp.sum(product * product, axis=0), 'mp')  19.4 us
    another operation x1, local copies, waits for them, and re-layouts, per_device(): stacked = jnp.stack(w_parts, axis=0)  17.8 us
    all_to_all x1, local copies, waits for them, and re-layouts, per_device(): lax.all_to_all(stacked, 'mp', split_axis=2, concat_axis=1, tiled=True)  13.6 us
    all_to_all x1, waiting for transfers between devices, per_device(): lax.all_to_all(stacked, 'mp', split_axis=2, concat_axis=1, tiled=True)  8.12 us
    all_to_all x1, starting transfers between devices, per_device(): lax.all_to_all(stacked, 'mp', split_axis=2, concat_axis=1, tiled=True)  7.44 us
  transfers between devices with their start and end apart: 2, of which 2 were waited for; matrix products, arithmetic and copies ran while one was open for 0% of the time, Pallas kernels for 0%

commit v1 on v0

v1 whole, which is shorter than its diff:
```python
import jax
import jax.numpy as jnp
from jax import lax
from jax.sharding import PartitionSpec as P

epsilon = 1e-06


def split_two(values):
    scaled = values * 128.0
    first = jnp.floor(scaled)
    second = jnp.floor((scaled - first) * 256.0)
    return first, second


def matmul(w_side, x_side):
    return lax.dot_general(
        w_side, x_side, (((1,), (1,)), ((), ())), preferred_element_type=jnp.float32
    )


def unite(first, second):
    return first * 256.0 + second


def part_again(united):
    first = jnp.floor(united * (1.0 / 256.0))
    second = united - first * 256.0
    return first.astype(jnp.bfloat16), second.astype(jnp.bfloat16)


def partial_rows(united, x_parts):
    w_first, w_second = part_again(united)
    level_zero = matmul(w_first, x_parts[0])
    level_one = matmul(w_first, x_parts[1]) + matmul(w_second, x_parts[0])
    return level_zero + level_one / 256.0


def per_device(inputs, weight):
    n_mp = lax.axis_size("mp")
    n_rows = lax.axis_size("rows")
    at = lax.axis_index("rows")
    cols, inner = weight.shape
    rows, block = inputs.shape
    share = cols // n_rows

    mine = lax.dynamic_slice_in_dim(weight, at * share, share, axis=0)
    mine_scale = jnp.max(jnp.abs(mine), axis=1) + epsilon
    united = unite(*split_two(mine / mine_scale[:, None]))
    send = united.reshape(share, n_mp, block).transpose(1, 0, 2)
    moved = lax.all_to_all(send, "mp", split_axis=0, concat_axis=0, tiled=True)
    held = [moved.reshape(n_mp * share, block)]
    step = n_rows // 2
    order = [0]
    while step:
        pairs = [(i, i ^ step) for i in range(n_rows)]
        held = held + [lax.ppermute(part, "rows", pairs) for part in held]
        order = order + [spot ^ step for spot in order]
        step //= 2

    row_max = lax.all_gather(jnp.max(jnp.abs(inputs), axis=1), "mp")
    row_scale = jnp.max(row_max, axis=0) + epsilon
    x_parts = tuple(
        part.astype(jnp.bfloat16) for part in split_two(inputs / row_scale[:, None])
    )
    terms = [partial_rows(part, x_parts).reshape(n_mp, 1, share, rows) for part in held]
    blocks = lax.all_to_all(
        jnp.concatenate(terms, axis=1), "mp", split_axis=0, concat_axis=0, tiled=True
    )
    combined = jnp.sum(blocks, axis=0)
    spots = [order.index(i) for i in range(n_rows)]
    step = 1
    while step < n_rows:
        flipped = jnp.stack([combined[order.index(order[i] ^ step)] for i in range(n_rows)])
        combined = jnp.where((at & step) != 0, flipped, combined)
        step *= 2
    combined = jnp.concatenate([combined[i] for i in spots], axis=0)

    col_scale = jnp.max(jnp.abs(weight), axis=1) + epsilon
    product = combined * col_scale[:, None] * row_scale[None, :] / inner
    squares = lax.all_gather(jnp.sum(product * product, axis=0), ("mp", "rows"))
    squares = jnp.sum(squares.reshape(n_mp, n_rows, rows), axis=0)
    mean_square = squares / (cols * n_mp)
    inverse = lax.rsqrt(mean_square + epsilon)
    gathered = lax.all_gather(product, "rows")
    normalized = (gathered * inverse[:, None, :]).transpose(1, 0, 2)
    return row_scale, product, normalized.reshape(cols, n_rows * rows)


def solution(mesh):
    return jax.shard_map(
        per_device,
        mesh=mesh,
        in_specs=(P("rows", "mp"), P("mp", None)),
        out_specs=(P("rows"), P("mp", "rows"), P("mp", None)),
        check_vma=False,
    )
```

time: 283 us -> 141 us (0.50)
  local copies, waits for them, and re-layouts: 58.7 us -> 2.99 us
  waiting for transfers between devices: 78.6 us -> 30.2 us
  blocking collectives: 110 us -> 76.9 us
  between operations: 14.1 us -> 0.87 us
  starting transfers between devices: 7.48 us -> 15.7 us
    pmax x1 -> x0, blocking collectives: 85 us -> none  [per_device(): row_scale = lax.pmax(jnp.max(jnp.abs(inputs), axis=1), 'mp') + epsilon]
    all_gather x1 -> x3, blocking collectives: 5.78 us -> 76.9 us  [the longest x1 39.6 us: per_device(): squares = lax.all_gather(jnp.sum(product * product, axis=0), ('mp', 'rows'))]
    reduce_scatter x1 -> x0, waiting for transfers between devices: 70.5 us -> none  [per_device(): lax.psum_scatter(partial_term, 'mp', scatter_dimension=0, tiled=True)]
    unnamed x9 -> x5, local copies, waits for them, and re-layouts: 22.3 us -> 0.62 us
    psum x1 -> x0, blocking collectives: 19.4 us -> none  [per_device(): squares = lax.psum(jnp.sum(product * product, axis=0), 'mp')]
    another operation x1 -> x0, local copies, waits for them, and re-layouts: 17.8 us -> none  [per_device(): stacked = jnp.stack(w_parts, axis=0)]
    ppermute x0 -> x3, waiting for transfers between devices: none -> 17.5 us  [per_device(): held = held + [lax.ppermute(part, 'rows', pairs) for part in held]]
    all_to_all x1 -> x0, local copies, waits for them, and re-layouts: 13.6 us -> none  [per_device(): lax.all_to_all(stacked, 'mp', split_axis=2, concat_axis=1, tiled=True)]
  transfers between devices with their start and end apart: 2 -> 5, of which waited for: 2 -> 2; matrix products, arithmetic and copies ran while one was open for 0% -> 6% of each run, Pallas kernels for 0% -> 0%
where the time goes in v1:
time: 141 us
  blocking collectives  76.9 us (55%)
  waiting for transfers between devices  30.2 us (21%)
  starting transfers between devices  15.7 us (11%)
  other arithmetic  8.16 us (6%)
  matrix products  5.95 us (4%)
  local copies, waits for them, and re-layouts  2.99 us (2%)
    all_gather x1, blocking collectives, per_device(): squares = lax.all_gather(jnp.sum(product * product, axis=0), ('mp', 'rows'))  39.6 us
    all_gather x1, blocking collectives, per_device(): row_max = lax.all_gather(jnp.max(jnp.abs(inputs), axis=1), 'mp')  31.5 us
    ppermute x3, waiting for transfers between devices, per_device(): held = held + [lax.ppermute(part, 'rows', pairs) for part in held]  17.5 us
    all_to_all x1, waiting for transfers between devices, per_device(): lax.all_to_all(jnp.concatenate(terms, axis=1), 'mp', split_axis=0, concat...  12.7 us
    all_to_all x1, starting transfers between devices, per_device(): moved = lax.all_to_all(send, 'mp', split_axis=0, concat_axis=0, tiled=True)  7.31 us
    all_to_all x1, starting transfers between devices, per_device(): lax.all_to_all(jnp.concatenate(terms, axis=1), 'mp', split_axis=0, concat...  6.82 us
    dot_general x12, matrix products, matmul(): lax.dot_general(w_side, x_side, (((1,), (1,)), ((), ())), preferred_eleme...  5.95 us
    all_gather x1, blocking collectives, per_device(): gathered = lax.all_gather(product, 'rows')  5.78 us
  transfers between devices with their start and end apart: 5, of which 2 were waited for; matrix products, arithmetic and copies ran while one was open for 6% of the time, Pallas kernels for 0%

profile of v1, /device:TPU:0, one launch (start us, length us, event | category | flops | bytes accessed | tf_op | source)
XLA Modules:
  0.0 140.8 jit_solution(10220289273291560609)
XLA Ops:
  0.6 1.4 abs_reduce_fusion.2
  2.0 1.6 %fusion.8 = f32[16,16384]{1,0:T(8,128)S(1)} fusion(f32[64,16384]{1,0:T(8,128)} %param.3, s32[]{:T(128)S(6)} %select_n.19, f32[16]{0:T(128)S(1)} %broadcast_add_fusion.2), kind=kLoop, calls=%fused_computation.22 | loop fusion | flops 2097152 | bytes 2097220 | tf_op jit(solution)/shard_map/add | solution.py:23
  3.6 0.6 copy.22
  4.2 0.0 copy-start
  4.2 1.6 %copy.14 = f32[8,16,2048]{2,1,0:T(8,128)} copy(f32[8,16,2048]{2,0,1:T(8,128)S(1)} %bitcast.48) | data formatting | bytes 2097152 | tf_op jit(solution)/shard_map/transpose | solution.py:50
  5.8 7.3 %all-to-all-start = ((f32[8,16,2048]{2,1,0:T(8,128)}), f32[8,16,2048]{2,1,0:T(8,128)S(1)}, u32[]{:S(2)}, u32[]{:S(2)}) async-start(f32[8,16,2048]{2,1,0:T(8,128)} %copy.14), calls=%async_computation | async-start | bytes 2097152 | tf_op jit(solution)/shard_map/all_to_all | solution.py:51
  13.1 0.0 copy-done
  13.2 0.2 abs_reduce_fusion.1
  13.4 31.5 %all-gather.2 = f32[8,1,256]{2,1,0:T(1,128)S(1)} all-gather(f32[1,1,256]{2,1,0:T(1,128)S(1)} %bitcast.56), channel_id=2, replica_groups=mesh['mp'=8,'rows'=4] {'mp'}, dimensions={0}, use_global_device_ids=true | all-gather | bytes 9216 | tf_op jit(solution)/shard_map/all_gather | solution.py:61
  44.9 0.0 copy-start.1
  44.9 0.0 all-to-all-done
  45.0 1.6 %collective-permute-start = (f32[128,2048]{1,0:T(8,128)S(1)}, f32[128,2048]{1,0:T(8,128)S(1)}, u32[]{:S(2)}, u32[]{:S(2)}) collective-permute-start(f32[128,2048]{1,0:T(8,128)S(1)} %bitcast.43), channel_id=1, source_target_pairs={{0,2},{1,3},{2,0},{3,1},{4,6},{5,7},{6,4},{7,5},{8,10},{9,11},{10,... | collective-permute-start | bytes 3145736 | tf_op jit(solution)/shard_map/ppermute | solution.py:57
  46.5 0.0 collective-permute-start.1
  46.5 0.6 fusion.2
  47.1 0.5 fusion.28
  47.6 0.5 fusion.26
  48.1 0.5 fusion.7
  48.7 17.5 %collective-permute-done = f32[128,2048]{1,0:T(8,128)S(1)} collective-permute-done((f32[128,2048]{1,0:T(8,128)S(1)}, f32[128,2048]{1,0:T(8,128)S(1)}, u32[]{:S(2)}, u32[]{:S(2)}) %collective-permute-start) | collective-permute-done | bytes 1048608 | tf_op jit(solution)/shard_map/ppermute | solution.py:57
  66.2 0.0 collective-permute-start.2
  66.2 0.0 collective-permute-done.1
  66.2 0.5 fusion.16
  66.7 0.5 fusion.4
  67.2 0.5 fusion.15
  67.7 0.5 convolution_add_fusion.3
  68.2 0.5 fusion.5
  68.7 0.5 convolution_add_fusion.5
  69.2 0.0 collective-permute-done.2
  69.2 0.5 fusion.17
  69.7 0.5 fusion.3
  70.2 0.5 convolution_add_fusion.1
  70.7 0.8 pad_maximum_fusion
  71.5 6.8 %all-to-all-start.1 = ((f32[8,4,16,256]{3,2,1,0:T(8,128)}), f32[8,4,16,256]{3,2,1,0:T(8,128)S(1)}, u32[]{:S(2)}, u32[]{:S(2)}) async-start(f32[8,4,16,256]{3,2,1,0:T(8,128)} %pad_maximum_fusion), calls=%async_computation.1 | async-start | bytes 1048576 | tf_op jit(solution)/shard_map/all_to_all | solution.py:67
  78.4 2.5 %abs_reduce_fusion = f32[64]{0:T(128)S(1)} fusion(f32[64,16384]{1,0:T(8,128)} %param.3), kind=kLoop, calls=%fused_computation | loop fusion | flops 2097088 | bytes 4194560 | tf_op jit(solution)/shard_map/reduce_max | solution.py:79
  80.9 12.7 %all-to-all-done.1 = f32[8,4,16,256]{3,2,1,0:T(8,128)S(1)} async-done(((f32[8,4,16,256]{3,2,1,0:T(8,128)}), f32[8,4,16,256]{3,2,1,0:T(8,128)S(1)}, u32[]{:S(2)}, u32[]{:S(2)}) %all-to-all-start.1) | async-done | bytes 524320 | tf_op jit(solution)/shard_map/all_to_all | solution.py:67
  93.7 0.1 fusion.39
  93.8 5.8 %all_gather.18 = f32[4,64,256]{2,1,0:T(8,128)S(1)} all-gather(f32[1,64,256]{2,1,0:T(8,128)S(1)} %fusion.39), channel_id=1, replica_groups=mesh['mp'=8,'rows'=4] {'rows'}, dimensions={0}, use_global_device_ids=true | all-gather | bytes 327680 | tf_op jit(solution)/shard_map/all_gather | solution.py:85
  99.5 0.0 copy-done.1
  99.5 0.7 multiply_reduce_fusion
  100.2 39.6 %all-gather.3 = f32[32,1,256]{2,1,0:T(1,128)S(1)} all-gather(f32[1,1,256]{2,1,0:T(1,128)S(1)} %bitcast.55), channel_id=3, replica_groups=mesh['mp'=8,'rows'=4] {'mp','rows'}, dimensions={0}, use_global_device_ids=true | all-gather | bytes 33792 | tf_op jit(solution)/shard_map/all_gather | solution.py:81
  139.9 0.1 reduce.1
  140.0 0.7 copy.21
  (14 shorter events, 0.2 us)
Async XLA Ops:
  4.2 8.9 %copy-start = (f32[256,2048]{1,0:T(8,128)S(1)}, f32[256,2048]{1,0:T(8,128)}, u32[]{:S(2)}) copy-start(f32[256,2048]{1,0:T(8,128)} %param.2) | copy-start | bytes 6291460
  5.8 39.1 %all-to-all-start = ((f32[8,16,2048]{2,1,0:T(8,128)}), f32[8,16,2048]{2,1,0:T(8,128)S(1)}, u32[]{:S(2)}, u32[]{:S(2)}) async-start(f32[8,16,2048]{2,1,0:T(8,128)} %copy.14), calls=%async_computation | async-start | bytes 2097152 | tf_op jit(solution)/shard_map/all_to_all | solution.py:51
  44.9 54.6 %copy-start.1 = (f32[256]{0:T(256)}, f32[256]{0:T(256)S(1)}, u32[]{:S(2)}) copy-start(f32[256]{0:T(256)S(1)} %broadcast_add_fusion) | copy-start | bytes 3076
  45.0 21.2 %collective-permute-start = (f32[128,2048]{1,0:T(8,128)S(1)}, f32[128,2048]{1,0:T(8,128)S(1)}, u32[]{:S(2)}, u32[]{:S(2)}) collective-permute-start(f32[128,2048]{1,0:T(8,128)S(1)} %bitcast.43), channel_id=1, source_target_pairs={{0,2},{1,3},{2,0},{3,1},{4,6},{5,7},{6,4},{7,5},{8,10},{9,11},{10,... | collective-permute-start | bytes 3145736 | tf_op jit(solution)/shard_map/ppermute | solution.py:57
  46.5 19.7 %collective-permute-start.1 = (f32[128,2048]{1,0:T(8,128)S(1)}, f32[128,2048]{1,0:T(8,128)S(1)}, u32[]{:S(2)}, u32[]{:S(2)}) collective-permute-start(f32[128,2048]{1,0:T(8,128)S(1)} %bitcast.44), channel_id=1, source_target_pairs={{0,1},{1,0},{2,3},{3,2},{4,5},{5,4},{6,7},{7,6},{8,9},{9,8},{10,11... | collective-permute-start | bytes 3145736 | tf_op jit(solution)/shard_map/ppermute | solution.py:57
  66.2 3.0 %collective-permute-start.2 = (f32[128,2048]{1,0:T(8,128)S(1)}, f32[128,2048]{1,0:T(8,128)S(1)}, u32[]{:S(2)}, u32[]{:S(2)}) collective-permute-start(f32[128,2048]{1,0:T(8,128)S(1)} %collective-permute-done), channel_id=1, source_target_pairs={{0,1},{1,0},{2,3},{3,2},{4,5},{5,4},{6,7},{7,6},{8,9},{9,8},{10,11... | collective-permute-start | bytes 3145736 | tf_op jit(solution)/shard_map/ppermute | solution.py:57
  71.5 22.0 %all-to-all-start.1 = ((f32[8,4,16,256]{3,2,1,0:T(8,128)}), f32[8,4,16,256]{3,2,1,0:T(8,128)S(1)}, u32[]{:S(2)}, u32[]{:S(2)}) async-start(f32[8,4,16,256]{3,2,1,0:T(8,128)} %pad_maximum_fusion), calls=%async_computation.1 | async-start | bytes 1048576 | tf_op jit(solution)/shard_map/all_to_all | solution.py:67
